TPU v7x, 32 devices: a whole 2x2x4 slice. The times are simulated.
32 devices in a mesh: freq: 4 (over y, x), row: 8 (over z, core).
Axes of the slice: x: 2, y: 2, z: 4, core: 2. Of those that a mesh axis runs over, the one named last changes fastest.
Arguments:
- data: bfloat16 [4, 2, 2048, 2048], P('freq', None, 'row'), may hold values from -60 to 60
Outputs:
- solution: float32 [4, 2, 2048, 2048], P('freq', None, 'row')
- direction: float32 [4, 2, 2048, 2048], P('freq', None, 'row')
All inputs are finite; a program needn't handle non-finite values.
Results may differ from a plain program's by a relative error of at most 0.0042.
Values may be sent and summed in bfloat16 or wider, within the bound.
A program may use at most 128 MiB of HBM per device.

v0:
```python
import functools

import jax
import jax.numpy as jnp
from jax import lax
from jax.experimental import pallas as pl
from jax.experimental.pallas import tpu as pltpu
from jax.sharding import PartitionSpec as P

ITERS = 2
MESH = pl.DeviceIdType.MESH
F32 = jnp.float32
BF16 = jnp.bfloat16


def dot(a, b):
    return lax.dot_general(a, b, (((1,), (0,)), ((), ())), preferred_element_type=F32)


def dot_t(a, b):
    return lax.dot_general(a, b, (((1,), (1,)), ((), ())), preferred_element_type=F32)


def lane_sums(x):
    s = jnp.sum(x, axis=0, keepdims=True)
    return functools.reduce(jnp.add, [s[:, i : i + 128] for i in range(0, s.shape[1], 128)])


def kernel(
    n, nf, weight, data, *refs,
):
    outs, refs = refs[: ITERS + 1], refs[ITERS + 1 :]
    coef, refs = refs[0], refs[1:]
    models, refs = refs[:ITERS], refs[ITERS:]
    (
        full, va, vd, d_raw, image, work, stats, slots, sums, fslots,
        load_sem, ssem, rsem, st_s, st_r, sf_s, sf_r, model_sem, image_sem,
    ) = refs
    m_raw = models[0]
    rows, order = data.shape[2], data.shape[3]
    m = n // 2
    me = lax.axis_index("row")
    mf = lax.axis_index("freq")
    z, c = lax.div(me, 2), lax.rem(me, 2)
    overlap = rows % 128 == 0
    unit = rows if overlap else min(order, 256)
    wide = min(order // 2, 512)

    def at_row(r):
        return {"row": r}

    def halves(body, between):
        count = order // wide
        pl.loop(0, count // 2)(body)
        between()
        pl.loop(count // 2, count)(body)

    def leave_model(it, p):
        return pltpu.make_async_copy(
            models[it].at[pl.ds(p * rows, rows), :], outs[it].at[0, p], model_sem.at[it, p]
        )

    def leave_image(i, p):
        cols = pl.ds(pl.multiple_of(i * wide, wide), wide)
        return pltpu.make_async_copy(
            image.at[pl.ds(p * rows, rows), cols],
            outs[ITERS].at[0, p, :, cols],
            image_sem.at[i, p],
        )

    def piece(zb, cc, p):
        start = pl.multiple_of((zb * 2 + cc) * rows, rows)
        return full.at[p, pl.ds(start, rows), :]

    loads = []
    for p in range(2):
        loads.append(pltpu.make_async_copy(data.at[0, p], piece(z, c, p), load_sem.at[p]))
        loads.append(
            pltpu.make_async_copy(
                data.at[0, p], vd.at[pl.ds(p * rows, rows), :], load_sem.at[2 + p]
            )
        )
    for copy in loads:
        copy.start()

    barrier = pltpu.get_barrier_semaphore()

    @pl.loop(1, n)
    def _(k):
        pl.semaphore_signal(
            barrier, inc=1, device_id=at_row(lax.rem(me + k, n)), device_id_type=MESH
        )

    @pl.loop(1, nf)
    def _(k):
        pl.semaphore_signal(
            barrier, inc=1, device_id={"freq": lax.rem(mf + k, nf)}, device_id_type=MESH
        )

    for copy in loads:
        copy.wait()

    stats[...] = jnp.zeros_like(stats)
    pl.semaphore_wait(barrier, n - 1 + nf - 1)

    def row_stat(k, j):
        return pltpu.make_async_remote_copy(
            src_ref=stats.at[k], dst_ref=slots.at[k, me], send_sem=st_s.at[k, j],
            recv_sem=st_r.at[k, me], device_id=at_row(j), device_id_type=MESH,
        )

    def row_arrival(k, j):
        return pltpu.make_async_remote_copy(
            src_ref=stats.at[k], dst_ref=slots.at[k, j], send_sem=st_s.at[k, j],
            recv_sem=st_r.at[k, j], device_id=at_row(j), device_id_type=MESH,
        )

    def freq_stat(k, j):
        return pltpu.make_async_remote_copy(
            src_ref=sums.at[k], dst_ref=fslots.at[k, mf], send_sem=sf_s.at[k, j],
            recv_sem=sf_r.at[k, mf], device_id={"freq": j}, device_id_type=MESH,
        )

    def freq_arrival(k, j):
        return pltpu.make_async_remote_copy(
            src_ref=sums.at[k], dst_ref=fslots.at[k, j], send_sem=sf_s.at[k, j],
            recv_sem=sf_r.at[k, j], device_id={"freq": j}, device_id_type=MESH,
        )

    def start_sum(k):
        slots[k, me] = stats[k]

        @pl.loop(1, n)
        def _(i):
            row_stat(k, lax.rem(me + i, n)).start()

    def middle_sum(k):
        @pl.loop(1, n)
        def _(i):
            row_arrival(k, lax.rem(me + i, n)).wait_recv()

        total = lax.fori_loop(
            1, n, lambda j, t: t + slots[k, j], slots[k, 0]
        )
        sums[k] = total
        fslots[k, mf] = total

        @pl.loop(1, nf)
        def _(i):
            freq_stat(k, lax.rem(mf + i, nf)).start()

    def finish_sum(k):
        @pl.loop(1, nf)
        def _(i):
            freq_arrival(k, lax.rem(mf + i, nf)).wait_recv()

        total = lax.fori_loop(
            1, nf, lambda j, t: t + fslots[k, j], fslots[k, 0]
        )
        values = jnp.sum(total, axis=1, keepdims=True)
        return [values[q : q + 1, :] for q in range(4)]

    def drain_sum(k):
        @pl.loop(1, n)
        def _(i):
            row_stat(k, lax.rem(me + i, n)).wait_send()

        @pl.loop(1, nf)
        def _(i):
            freq_stat(k, lax.rem(mf + i, nf)).wait_send()

    def block_copy(lane, zb, cc, p, target):
        return pltpu.make_async_remote_copy(
            src_ref=piece(zb, cc, p), dst_ref=piece(zb, cc, p),
            send_sem=ssem.at[lane, zb, p], recv_sem=rsem.at[zb * 2 + cc, p],
            device_id=at_row(target), device_id_type=MESH,
        )

    sibling = z * 2 + (1 - c)

    def spread(zb, p, below, above):
        @pl.when(below & (z + 1 < m))
        def _():
            block_copy(0, zb, c, p, lax.rem(me + 2, n)).start()

        @pl.when(above & (z > 0))
        def _():
            block_copy(1, zb, c, p, lax.rem(me + n - 2, n)).start()

        block_copy(2, zb, c, p, sibling).start()

    def settle(zb, p):
        @pl.when((zb <= z) & (z + 1 < m))
        def _():
            block_copy(0, zb, c, p, lax.rem(me + 2, n)).wait_send()

        @pl.when((zb >= z) & (z > 0))
        def _():
            block_copy(1, zb, c, p, lax.rem(me + n - 2, n)).wait_send()

        block_copy(2, zb, c, p, sibling).wait_send()

    spread(z, 0, jnp.bool_(True), jnp.bool_(True))

    @pl.loop(0, order // wide)
    def _(i):
        x = vd[:, pl.ds(pl.multiple_of(i * wide, wide), wide)].astype(F32)
        stats[0, 0:1, :] += lane_sums(x * x)

    start_sum(0)
    spread(z, 1, jnp.bool_(True), jnp.bool_(True))

    @pl.loop(0, order // wide)
    def _(i):
        cols = pl.ds(pl.multiple_of(i * wide, wide), wide)
        work[:, cols] = jnp.zeros((2 * rows, wide), F32)

    middle_sum(0)
    beta = jnp.sqrt(finish_sum(0)[0])

    def process(start):
        band = pl.ds(pl.multiple_of(start, unit), unit)
        tr = dot_t(vd[...], full[0, band, :])
        ti = dot_t(vd[...], full[1, band, :])
        fit = jnp.concatenate([tr[:rows] + ti[rows:], tr[rows:] - ti[:rows]], axis=0)
        raw = (vd[:, band].astype(F32) - weight * fit) / beta
        m_raw[:, band] = raw
        stats[1, 0:1, :] += lane_sums(raw * raw)
        va[:, band] = raw.astype(BF16)

        @pl.loop(0, order // wide)
        def _(i):
            cols = pl.ds(pl.multiple_of(i * wide, wide), wide)
            v = va[:, band]
            a = dot(v, full[0, band, cols])
            b = dot(v, full[1, band, cols])
            work[:, cols] += jnp.concatenate(
                [a[:rows] - b[rows:], a[rows:] + b[:rows]], axis=0
            )

    @pl.loop(0, m)
    def _(s):
        @pl.when(s > 0)
        def _():
            for p in range(2):
                @pl.when(z - s >= 0)
                def _():
                    block_copy(0, z - s, c, p, sibling).wait_recv()
                    spread(z - s, p, jnp.bool_(True), jnp.bool_(False))

                @pl.when(z + s < m)
                def _():
                    block_copy(0, z + s, c, p, sibling).wait_recv()
                    spread(z + s, p, jnp.bool_(False), jnp.bool_(True))

        @pl.loop(0, 4)
        def _(t):
            up = lax.div(t, 2)
            other = lax.rem(t, 2)
            zb = z - s + 2 * s * up
            cc = c + other * (1 - 2 * c)

            @pl.when((zb >= 0) & (zb < m) & ((s > 0) | (t < 2)))
            def _():
                @pl.when(other == 1)
                def _():
                    for p in range(2):
                        block_copy(0, zb, cc, p, sibling).wait_recv()

                if overlap:
                    process((zb * 2 + cc) * rows)

    if not overlap:
        @pl.loop(0, order // unit)
        def _(u):
            process(u * unit)

    start_sum(1)
    for p in range(2):
        leave_model(0, p).start()
    middle_sum(1)
    alpha = jnp.sqrt(finish_sum(1)[0])

    phi_bar, rho_bar = beta, alpha
    direction, answer = [1.0 / alpha], []
    for it in range(ITERS):
        last = it == ITERS - 1
        model_ref = models[it]
        ka, kb = 2 * it + 1, 2 * it + 2

        if it > 0:
            def forward(i):
                cols = pl.ds(pl.multiple_of(i * wide, wide), wide)
                a = dot(va[...], full[0, :, cols])
                b = dot(va[...], full[1, :, cols])
                work[:, cols] = jnp.concatenate(
                    [a[:rows] - b[rows:], a[rows:] + b[:rows]], axis=0
                )

            halves(forward, lambda: middle_sum(ka))
            alpha = jnp.sqrt(finish_sum(ka)[0])
            rotate(alpha)
        inv_alpha, keep = 1.0 / alpha, alpha / beta

        @pl.loop(0, order // wide)
        def _(i):
            cols = pl.ds(pl.multiple_of(i * wide, wide), wide)
            old = vd[:, cols].astype(F32) if it == 0 else d_raw[:, cols]
            new = (model_ref[:, cols] - weight * work[:, cols]) * inv_alpha - keep * old
            d_raw[:, cols] = new
            vd[:, cols] = new.astype(BF16)
            stats[kb, 0:1, :] += lane_sums(new * new)

        start_sum(kb)

        def adjoint(i):
            cols = pl.ds(pl.multiple_of(i * wide, wide), wide)
            tr = dot_t(vd[...], full[0, cols, :])
            ti = dot_t(vd[...], full[1, cols, :])
            fit = jnp.concatenate([tr[:rows] + ti[rows:], tr[rows:] - ti[:rows]], axis=0)
            new = d_raw[:, cols] - weight * fit
            image[:, cols] = new
            if last:
                stats[kb + 1, 0:1, :] += lane_sums(new * new)
                stats[kb + 1, 1:2, :] += lane_sums(new * model_ref[:, cols])
                for p in range(2):
                    leave_image(i, p).start()

        halves(adjoint, lambda: middle_sum(kb))
        if last:
            start_sum(kb + 1)
        data_sq = finish_sum(kb)[0]
        beta = jnp.sqrt(data_sq)
        inv_beta, shift = 1.0 / beta, beta / alpha

        if not last:
            @pl.loop(0, order // wide)
            def _(i):
                cols = pl.ds(pl.multiple_of(i * wide, wide), wide)
                new = image[:, cols] * inv_beta - shift * model_ref[:, cols]
                models[it + 1][:, cols] = new
                va[:, cols] = new.astype(BF16)
                stats[kb + 1, 0:1, :] += lane_sums(new * new)

            start_sum(kb + 1)
            for p in range(2):
                leave_model(it + 1, p).start()

        rho = jnp.sqrt(rho_bar * rho_bar + beta * beta)
        cosine, sine = rho_bar / rho, beta / rho
        step = cosine * phi_bar / rho
        phi_bar = sine * phi_bar
        answer = [x + step * w for x, w in zip(answer + [0.0], direction)]

        def rotate(alpha, sine=sine, cosine=cosine, rho=rho):
            nonlocal rho_bar, direction
            rho_bar = -cosine * alpha
            turn = sine * alpha / rho
            direction = [-turn * w for w in direction] + [1.0 / alpha]

    middle_sum(kb + 1)
    image_sq, cross = finish_sum(kb + 1)[:2]
    new_alpha = jnp.sqrt(image_sq / data_sq - 2.0 * cross / alpha + data_sq)
    rotate(new_alpha)
    tip = direction.pop()
    direction[-1] = direction[-1] - tip * shift
    direction.append(tip * inv_beta)
    for q, value in enumerate(answer + direction):
        coef[q : q + 1, :] = jnp.broadcast_to(value, (1, 128))

    for k in range(2 + 2 * ITERS):
        drain_sum(k)

    @pl.loop(0, m)
    def _(zb):
        for p in range(2):
            settle(zb, p)

    for p in range(2):
        for it in range(ITERS):
            leave_model(it, p).wait()

        @pl.loop(0, order // wide)
        def _(i):
            leave_image(i, p).wait()


def on_device(n, nf, data):
    rows, order = data.shape[2], data.shape[3]
    weight = 1.0 / (3.0 * (2.0 * order) ** 0.5)
    field = pltpu.VMEM((2 * rows, order), F32)
    rounded = pltpu.VMEM((2 * rows, order), BF16)
    rounds = 2 + 2 * ITERS
    dma = pltpu.SemaphoreType.DMA
    out = jax.ShapeDtypeStruct(data.shape, F32)
    anywhere = pl.BlockSpec(memory_space=pl.ANY)
    *basis, coef = pl.pallas_call(
        functools.partial(kernel, n, nf, weight),
        out_shape=(out,) * (ITERS + 1) + (jax.ShapeDtypeStruct((2 * ITERS + 1, 128), F32),),
        in_specs=[anywhere],
        out_specs=(anywhere,) * (ITERS + 1) + (pl.BlockSpec(memory_space=pltpu.VMEM),),
        scratch_shapes=[field] * ITERS
        + [
            pltpu.VMEM((2, order, order), BF16),
            rounded, rounded, field, field, field,
            pltpu.VMEM((rounds, 8, 128), F32),
            pltpu.VMEM((rounds, n, 8, 128), F32),
            pltpu.VMEM((rounds, 8, 128), F32),
            pltpu.VMEM((rounds, nf, 8, 128), F32),
            dma((4,)), dma((3, n // 2, 2)), dma((n, 2)),
            dma((rounds, n)), dma((rounds, n)),
            dma((rounds, nf)), dma((rounds, nf)),
            dma((ITERS, 2)), dma((max(2, order // 512), 2)),
        ],
        compiler_params=pltpu.CompilerParams(
            collective_id=0, has_side_effects=True, vmem_limit_bytes=60 * 2**20
        ),
    )(data)
    answer = sum(coef[k, 0] * basis[k] for k in range(ITERS))
    direction = sum(coef[ITERS + k, 0] * basis[k] for k in range(ITERS + 1))
    return answer, direction


def solution(mesh):
    spec = P("freq", None, "row", None)
    return jax.shard_map(
        functools.partial(on_device, mesh.shape["row"], mesh.shape["freq"]),
        mesh=mesh,
        in_specs=(spec,),
        out_specs=(spec, spec),
        check_vma=False,
    )
```

profile of v0, /device:TPU:0, one launch (start us, length us, event | category | flops | bytes accessed | tf_op | source)
XLA Modules:
  0.0 214.9 jit_solution(1667738800422222383)
XLA Ops:
  0.6 199.2 %shard_map.30 = (f32[1,2,256,2048]{3,2,1,0:T(8,128)}, f32[1,2,256,2048]{3,2,1,0:T(8,128)}, f32[1,2,256,2048]{3,2,1,0:T(8,128)}, f32[5,128]{1,0:T(8,128)}) custom-call(bf16[1,2,256,2048]{3,2,1,0:T(8,128)(2,1)} %data.1), custom_call_target="tpu_custom_call" | custom-call | tf_op jit(solution)/shard_map/pallas_call | solution.py:397
  199.9 1.4 fusion
  201.3 13.6 %multiply_add_fusion = (f32[1,2,256,2048]{3,2,1,0:T(8,128)}, f32[1,2,256,2048]{3,2,1,0:T(8,128)}) fusion(f32[1,2,256,2048]{3,2,1,0:T(8,128)} %get-tuple-element.9, f32[1,2,256,2048]{3,2,1,0:T(8,128)} %get-tuple-element.8, f32[1,2,256,2048]{3,2,1,0:T(8,128)} %get-tuple-element.7, f32[]{:T(128)} %bitcast.4, f32[]{:T(128)} %bitcast.3, f32[]{:T(128)} %bitcast.2, ...), kind=kLoop, calls=%fused_computation | loop fusion | flops 8388608 | bytes 20971540 | tf_op jit(solution)/shard_map/add | solution.py:420
where the time goes:
time: 215 us
  Pallas kernels  199 us (93%)
  other arithmetic  13.6 us (6%)
    pallas_call x1, Pallas kernels, on_device(): pl.pallas_call(functools.partial(kernel, n, nf, weight), out_shape=(out,)...  199 us
    add x1, other arithmetic, on_device(): direction = sum((coef[ITERS + k, 0] * basis[k] for k in range(ITERS + 1)))  13.6 us

commit v1 on v0

--- a/solution.py
+++ b/solution.py
@@ -29,12 +29,10 @@
 def kernel(
     n, nf, weight, data, *refs,
 ):
-    outs, refs = refs[: ITERS + 1], refs[ITERS + 1 :]
-    coef, refs = refs[0], refs[1:]
-    models, refs = refs[:ITERS], refs[ITERS:]
+    models, image, coef, refs = refs[:ITERS], refs[ITERS], refs[ITERS + 1], refs[ITERS + 2 :]
     (
-        full, va, vd, d_raw, image, work, stats, slots, sums, fslots,
-        load_sem, ssem, rsem, st_s, st_r, sf_s, sf_r, model_sem, image_sem,
+        full, va, vd, d_raw, work, stats, slots, sums, fslots,
+        load_sem, ssem, rsem, st_s, st_r, sf_s, sf_r,
     ) = refs
     m_raw = models[0]
     rows, order = data.shape[2], data.shape[3]
@@ -55,19 +53,6 @@
         between()
         pl.loop(count // 2, count)(body)
 
-    def leave_model(it, p):
-        return pltpu.make_async_copy(
-            models[it].at[pl.ds(p * rows, rows), :], outs[it].at[0, p], model_sem.at[it, p]
-        )
-
-    def leave_image(i, p):
-        cols = pl.ds(pl.multiple_of(i * wide, wide), wide)
-        return pltpu.make_async_copy(
-            image.at[pl.ds(p * rows, rows), cols],
-            outs[ITERS].at[0, p, :, cols],
-            image_sem.at[i, p],
-        )
-
     def piece(zb, cc, p):
         start = pl.multiple_of((zb * 2 + cc) * rows, rows)
         return full.at[p, pl.ds(start, rows), :]
@@ -276,8 +261,6 @@
             process(u * unit)
 
     start_sum(1)
-    for p in range(2):
-        leave_model(0, p).start()
     middle_sum(1)
     alpha = jnp.sqrt(finish_sum(1)[0])
 
@@ -323,8 +306,6 @@
             if last:
                 stats[kb + 1, 0:1, :] += lane_sums(new * new)
                 stats[kb + 1, 1:2, :] += lane_sums(new * model_ref[:, cols])
-                for p in range(2):
-                    leave_image(i, p).start()
 
         halves(adjoint, lambda: middle_sum(kb))
         if last:
@@ -343,8 +324,6 @@
                 stats[kb + 1, 0:1, :] += lane_sums(new * new)
 
             start_sum(kb + 1)
-            for p in range(2):
-                leave_model(it + 1, p).start()
 
         rho = jnp.sqrt(rho_bar * rho_bar + beta * beta)
         cosine, sine = rho_bar / rho, beta / rho
@@ -376,13 +355,36 @@
         for p in range(2):
             settle(zb, p)
 
+
+def combine(coef, *refs):
+    basis, refs = refs[: ITERS + 1], refs[ITERS + 1 :]
+    answer, direction, staged, sem = refs
+    rows, order = answer.shape[2], answer.shape[3]
+    high = min(rows, 64)
+    per = rows // high
+
+    def leave(t):
+        out = (answer, direction)[t[0]]
+        return pltpu.make_async_copy(
+            staged.at[t[0], pl.ds(t[1] * rows + t[2] * high, high), :],
+            out.at[0, t[1], pl.ds(t[2] * high, high), :],
+            sem.at[t],
+        )
+
+    factors = [coef[q : q + 1, 0:1] for q in range(2 * ITERS + 1)]
+    tiles = [(o, p, i) for p in range(2) for i in range(per) for o in range(2)]
     for p in range(2):
-        for it in range(ITERS):
-            leave_model(it, p).wait()
-
-        @pl.loop(0, order // wide)
-        def _(i):
-            leave_image(i, p).wait()
+        for i in range(per):
+            band = pl.ds(p * rows + i * high, high)
+            parts = [b[band, :] for b in basis]
+            for o in range(2):
+                used = parts[: ITERS + o]
+                staged[o, band, :] = sum(
+                    factors[o * ITERS + k] * x for k, x in enumerate(used)
+                )
+                leave((o, p, i)).start()
+    for t in tiles:
+        leave(t).wait()
 
 
 def on_device(n, nf, data):
@@ -392,17 +394,16 @@
     rounded = pltpu.VMEM((2 * rows, order), BF16)
     rounds = 2 + 2 * ITERS
     dma = pltpu.SemaphoreType.DMA
-    out = jax.ShapeDtypeStruct(data.shape, F32)
+    vmem = pl.BlockSpec(memory_space=pltpu.VMEM)
     anywhere = pl.BlockSpec(memory_space=pl.ANY)
     *basis, coef = pl.pallas_call(
         functools.partial(kernel, n, nf, weight),
-        out_shape=(out,) * (ITERS + 1) + (jax.ShapeDtypeStruct((2 * ITERS + 1, 128), F32),),
+        out_shape=(field,) * (ITERS + 1) + (pltpu.VMEM((8, 128), F32),),
         in_specs=[anywhere],
-        out_specs=(anywhere,) * (ITERS + 1) + (pl.BlockSpec(memory_space=pltpu.VMEM),),
-        scratch_shapes=[field] * ITERS
-        + [
+        out_specs=(vmem,) * (ITERS + 2),
+        scratch_shapes=[
             pltpu.VMEM((2, order, order), BF16),
-            rounded, rounded, field, field, field,
+            rounded, rounded, field, field,
             pltpu.VMEM((rounds, 8, 128), F32),
             pltpu.VMEM((rounds, n, 8, 128), F32),
             pltpu.VMEM((rounds, 8, 128), F32),
@@ -410,15 +411,21 @@
             dma((4,)), dma((3, n // 2, 2)), dma((n, 2)),
             dma((rounds, n)), dma((rounds, n)),
             dma((rounds, nf)), dma((rounds, nf)),
-            dma((ITERS, 2)), dma((max(2, order // 512), 2)),
         ],
         compiler_params=pltpu.CompilerParams(
-            collective_id=0, has_side_effects=True, vmem_limit_bytes=60 * 2**20
+            collective_id=0, has_side_effects=True, vmem_limit_bytes=46 * 2**20
         ),
     )(data)
-    answer = sum(coef[k, 0] * basis[k] for k in range(ITERS))
-    direction = sum(coef[ITERS + k, 0] * basis[k] for k in range(ITERS + 1))
-    return answer, direction
+    out = jax.ShapeDtypeStruct(data.shape, F32)
+    high = min(rows, 64)
+    return pl.pallas_call(
+        combine,
+        out_shape=(out, out),
+        in_specs=[vmem] * (ITERS + 2),
+        out_specs=(anywhere, anywhere),
+        scratch_shapes=[pltpu.VMEM((2, 2 * rows, order), F32), dma((2, 2, rows // high))],
+        compiler_params=pltpu.CompilerParams(vmem_limit_bytes=24 * 2**20),
+    )(coef, *basis)
 
 
 def solution(mesh):

time: 215 us -> 203 us (0.944)
  other arithmetic: 13.6 us -> 0 us
  Pallas kernels: 199 us -> 202 us
    add x1 -> x0, other arithmetic: 13.6 us -> none  [on_device(): direction = sum((coef[ITERS + k, 0] * basis[k] for k in range(ITERS + 1)))]
    pallas_call x1 -> x2, Pallas kernels: 199 us -> 202 us  [the longest x1 199 us: on_device(): pl.pallas_call(functools.partial(kernel, n, nf, weight), out_shape=(field...]
where the time goes in v1:
time: 203 us
  Pallas kernels  202 us (100%)
    pallas_call x1, Pallas kernels, on_device(): pl.pallas_call(functools.partial(kernel, n, nf, weight), out_shape=(field...  199 us

profile of v1, /device:TPU:0, one launch (start us, length us, event | category | flops | bytes accessed | tf_op | source)
XLA Modules:
  0.0 203.0 jit_solution(17729618679388917970)
XLA Ops:
  0.6 198.5 %shard_map.30 = (f32[512,2048]{1,0:T(8,128)S(1)}, f32[512,2048]{1,0:T(8,128)S(1)}, f32[512,2048]{1,0:T(8,128)S(1)}, f32[8,128]{1,0:T(8,128)S(1)}) custom-call(bf16[1,2,256,2048]{3,2,1,0:T(8,128)(2,1)} %data.1), custom_call_target="tpu_custom_call" | custom-call | tf_op jit(solution)/shard_map/pallas_call | solution.py:399
  199.2 3.7 %shard_map.31 = (f32[1,2,256,2048]{3,2,1,0:T(8,128)}, f32[1,2,256,2048]{3,2,1,0:T(8,128)}) custom-call(f32[8,128]{1,0:T(8,128)S(1)} %get-tuple-element.6.coef, f32[512,2048]{1,0:T(8,128)S(1)} %get-tuple-element.7.refs_0_, f32[512,2048]{1,0:T(8,128)S(1)} %get-tuple-element.8.refs_1_, f32[512,2048]{1,0:T(8,128)S(1)} %get-tuple-element.9.refs_2_), custom_call_target="tpu_custom_call" | custom-call | tf_op jit(solution)/shard_map/pallas_call | solution.py:421

commit v2 on v1

--- a/solution.py
+++ b/solution.py
@@ -32,7 +32,7 @@
     models, image, coef, refs = refs[:ITERS], refs[ITERS], refs[ITERS + 1], refs[ITERS + 2 :]
     (
         full, va, vd, d_raw, work, stats, slots, sums, fslots,
-        load_sem, ssem, rsem, st_s, st_r, sf_s, sf_r,
+        spot, seats, load_sem, ssem, rsem, st_s, st_r, sf_s, sf_r, cast_s, cast_r,
     ) = refs
     m_raw = models[0]
     rows, order = data.shape[2], data.shape[3]
@@ -43,6 +43,8 @@
     overlap = rows % 128 == 0
     unit = rows if overlap else min(order, 256)
     wide = min(order // 2, 512)
+    shadow = overlap and m >= 4
+    voters = range(2, n - 2) if shadow else range(n)
 
     def at_row(r):
         return {"row": r}
@@ -153,6 +155,48 @@
         @pl.loop(1, nf)
         def _(i):
             freq_stat(k, lax.rem(mf + i, nf)).wait_send()
+
+    def cast(k, j, g):
+        return pltpu.make_async_remote_copy(
+            src_ref=spot.at[k], dst_ref=seats.at[k, me * nf + mf],
+            send_sem=cast_s.at[k, j, g], recv_sem=cast_r.at[k, me, mf],
+            device_id={"row": j, "freq": g}, device_id_type=MESH,
+        )
+
+    def cast_arrival(k, j, g):
+        return pltpu.make_async_remote_copy(
+            src_ref=spot.at[k], dst_ref=seats.at[k, j * nf + g],
+            send_sem=cast_s.at[k, j, g], recv_sem=cast_r.at[k, j, g],
+            device_id={"row": j, "freq": g}, device_id_type=MESH,
+        )
+
+    def others(body):
+        @pl.loop(1, n * nf)
+        def _(i):
+            to = lax.rem(me * nf + mf + i, n * nf)
+            body(lax.div(to, nf), lax.rem(to, nf))
+
+    def start_cast(k, row):
+        values = jnp.sum(stats[row], axis=1, keepdims=True)
+        lane = lax.broadcasted_iota(jnp.int32, (1, 128), 1)
+        spot[k] = jnp.where(lane < 64, values[0:1], values[1:2])
+        seats[k, me * nf + mf] = spot[k]
+        others(lambda j, g: cast(k, j, g).start())
+
+    def finish_cast(k, rows_in):
+        @pl.loop(rows_in[0], rows_in[-1] + 1)
+        def _(j):
+            @pl.loop(0, nf)
+            def _(g):
+                @pl.when((j != me) | (g != mf))
+                def _():
+                    cast_arrival(k, j, g).wait_recv()
+
+        total = lax.fori_loop(
+            rows_in[0] * nf, (rows_in[-1] + 1) * nf,
+            lambda j, t: t + seats[k, j], jnp.zeros((1, 128), F32),
+        )
+        return total[:, 0:1], total[:, 64:65]
 
     def block_copy(lane, zb, cc, p, target):
         return pltpu.make_async_remote_copy(
@@ -260,9 +304,30 @@
         def _(u):
             process(u * unit)
 
-    start_sum(1)
-    middle_sum(1)
-    alpha = jnp.sqrt(finish_sum(1)[0])
+    if shadow:
+        @pl.when((z == 1) | (z == m - 2))
+        def _():
+            edge = jnp.where(z == 1, 0, m - 1)
+            vr, vi = piece(edge, c, 0), piece(edge, c, 1)
+
+            @pl.loop(0, order // unit)
+            def _(u):
+                band = pl.ds(pl.multiple_of(u * unit, unit), unit)
+                pr, pi = full.at[0, band, :], full.at[1, band, :]
+                fr = dot_t(vr[...], pr[...]) + dot_t(vi[...], pi[...])
+                raw = (vr[:, band].astype(F32) - weight * fr) / beta
+                stats[1, 0:1, :] += lane_sums(raw * raw)
+                fi = dot_t(vi[...], pr[...]) - dot_t(vr[...], pi[...])
+                raw = (vi[:, band].astype(F32) - weight * fi) / beta
+                stats[1, 0:1, :] += lane_sums(raw * raw)
+
+    votes = (me >= voters[0]) & (me <= voters[-1])
+
+    @pl.when(votes)
+    def _():
+        start_cast(0, 1)
+
+    alpha = jnp.sqrt(finish_cast(0, voters)[0])
 
     phi_bar, rho_bar = beta, alpha
     direction, answer = [1.0 / alpha], []
@@ -309,7 +374,7 @@
 
         halves(adjoint, lambda: middle_sum(kb))
         if last:
-            start_sum(kb + 1)
+            start_cast(1, kb + 1)
         data_sq = finish_sum(kb)[0]
         beta = jnp.sqrt(data_sq)
         inv_beta, shift = 1.0 / beta, beta / alpha
@@ -337,17 +402,15 @@
             turn = sine * alpha / rho
             direction = [-turn * w for w in direction] + [1.0 / alpha]
 
-    middle_sum(kb + 1)
-    image_sq, cross = finish_sum(kb + 1)[:2]
-    new_alpha = jnp.sqrt(image_sq / data_sq - 2.0 * cross / alpha + data_sq)
-    rotate(new_alpha)
-    tip = direction.pop()
-    direction[-1] = direction[-1] - tip * shift
-    direction.append(tip * inv_beta)
-    for q, value in enumerate(answer + direction):
-        coef[q : q + 1, :] = jnp.broadcast_to(value, (1, 128))
-
-    for k in range(2 + 2 * ITERS):
+    @pl.loop(0, order // wide)
+    def _(i):
+        cols = pl.ds(pl.multiple_of(i * wide, wide), wide)
+        parts = [model[:, cols] for model in models]
+        models[0][:, cols] = sum(w * x for w, x in zip(answer, parts))
+        models[1][:, cols] = sum(w * x for w, x in zip(direction, parts))
+        image[:, cols] = inv_beta * image[:, cols] - shift * parts[-1]
+
+    for k in (0, *range(2, 1 + 2 * ITERS)):
         drain_sum(k)
 
     @pl.loop(0, m)
@@ -355,36 +418,41 @@
         for p in range(2):
             settle(zb, p)
 
-
-def combine(coef, *refs):
-    basis, refs = refs[: ITERS + 1], refs[ITERS + 1 :]
-    answer, direction, staged, sem = refs
+    @pl.when(votes)
+    def _():
+        others(lambda j, g: cast(0, j, g).wait_send())
+
+    image_sq, cross = finish_cast(1, range(n))
+    new_alpha = jnp.sqrt(image_sq / data_sq - 2.0 * cross / alpha + data_sq)
+    coef[0:1, :] = jnp.broadcast_to(-sine * new_alpha / rho, (1, 128))
+    coef[1:2, :] = jnp.broadcast_to(1.0 / new_alpha, (1, 128))
+    others(lambda j, g: cast(1, j, g).wait_send())
+
+
+def combine(coef, ready, turned, fresh, answer, direction, staged, sem):
     rows, order = answer.shape[2], answer.shape[3]
     high = min(rows, 64)
     per = rows // high
 
-    def leave(t):
-        out = (answer, direction)[t[0]]
+    def leave(o, p, i):
+        source, out = ((ready, answer), (staged, direction))[o]
         return pltpu.make_async_copy(
-            staged.at[t[0], pl.ds(t[1] * rows + t[2] * high, high), :],
-            out.at[0, t[1], pl.ds(t[2] * high, high), :],
-            sem.at[t],
-        )
-
-    factors = [coef[q : q + 1, 0:1] for q in range(2 * ITERS + 1)]
-    tiles = [(o, p, i) for p in range(2) for i in range(per) for o in range(2)]
-    for p in range(2):
-        for i in range(per):
-            band = pl.ds(p * rows + i * high, high)
-            parts = [b[band, :] for b in basis]
-            for o in range(2):
-                used = parts[: ITERS + o]
-                staged[o, band, :] = sum(
-                    factors[o * ITERS + k] * x for k, x in enumerate(used)
-                )
-                leave((o, p, i)).start()
-    for t in tiles:
-        leave(t).wait()
+            source.at[pl.ds(p * rows + i * high, high), :],
+            out.at[0, p, pl.ds(i * high, high), :],
+            sem.at[o, p, i],
+        )
+
+    tiles = [(p, i) for p in range(2) for i in range(per)]
+    for p, i in tiles:
+        leave(0, p, i).start()
+    old, new = coef[0:1, 0:1], coef[1:2, 0:1]
+    for p, i in tiles:
+        band = pl.ds(p * rows + i * high, high)
+        staged[band, :] = old * turned[band, :] + new * fresh[band, :]
+        leave(1, p, i).start()
+    for p, i in tiles:
+        for o in range(2):
+            leave(o, p, i).wait()
 
 
 def on_device(n, nf, data):
@@ -408,9 +476,11 @@
             pltpu.VMEM((rounds, n, 8, 128), F32),
             pltpu.VMEM((rounds, 8, 128), F32),
             pltpu.VMEM((rounds, nf, 8, 128), F32),
+            pltpu.VMEM((2, 1, 128), F32), pltpu.VMEM((2, n * nf, 1, 128), F32),
             dma((4,)), dma((3, n // 2, 2)), dma((n, 2)),
             dma((rounds, n)), dma((rounds, n)),
             dma((rounds, nf)), dma((rounds, nf)),
+            dma((2, n, nf)), dma((2, n, nf)),
         ],
         compiler_params=pltpu.CompilerParams(
             collective_id=0, has_side_effects=True, vmem_limit_bytes=46 * 2**20
@@ -423,7 +493,7 @@
         out_shape=(out, out),
         in_specs=[vmem] * (ITERS + 2),
         out_specs=(anywhere, anywhere),
-        scratch_shapes=[pltpu.VMEM((2, 2 * rows, order), F32), dma((2, 2, rows // high))],
+        scratch_shapes=[pltpu.VMEM((2 * rows, order), F32), dma((2, 2, rows // high))],
         compiler_params=pltpu.CompilerParams(vmem_limit_bytes=24 * 2**20),
     )(coef, *basis)
 

time: 203 us -> 197 us (0.970)
  Pallas kernels: 202 us -> 196 us
    pallas_call x1, Pallas kernels: 199 us -> 193 us  [on_device(): pl.pallas_call(functools.partial(kernel, n, nf, weight), out_shape=(field...]
where the time goes in v2:
time: 197 us
  Pallas kernels  196 us (99%)
    pallas_call x1, Pallas kernels, on_device(): pl.pallas_call(functools.partial(kernel, n, nf, weight), out_shape=(field...  193 us

profile of v2, /device:TPU:0, one launch (start us, length us, event | category | flops | bytes accessed | tf_op | source)
XLA Modules:
  0.0 197.2 jit_solution(5315891687887434863)
XLA Ops:
  0.6 193.0 %shard_map.30 = (f32[512,2048]{1,0:T(8,128)S(1)}, f32[512,2048]{1,0:T(8,128)S(1)}, f32[512,2048]{1,0:T(8,128)S(1)}, f32[8,128]{1,0:T(8,128)S(1)}) custom-call(bf16[1,2,256,2048]{3,2,1,0:T(8,128)(2,1)} %data.1), custom_call_target="tpu_custom_call" | custom-call | tf_op jit(solution)/shard_map/pallas_call | solution.py:467
  193.6 3.4 %shard_map.31 = (f32[1,2,256,2048]{3,2,1,0:T(8,128)}, f32[1,2,256,2048]{3,2,1,0:T(8,128)}) custom-call(f32[8,128]{1,0:T(8,128)S(1)} %get-tuple-element.6.coef, f32[512,2048]{1,0:T(8,128)S(1)} %get-tuple-element.7.ready, f32[512,2048]{1,0:T(8,128)S(1)} %get-tuple-element.8.turned, f32[512,2048]{1,0:T(8,128)S(1)} %get-tuple-element.9.fresh), custom_call_target="tpu_custom_call" | custom-call | tf_op jit(solution)/shard_map/pallas_call | solution.py:491

commit v3 on v2

v3 whole, which is shorter than its diff:
```python
import functools

import jax
import jax.numpy as jnp
from jax import lax
from jax.experimental import pallas as pl
from jax.experimental.pallas import tpu as pltpu
from jax.sharding import PartitionSpec as P

ITERS = 2
MESH = pl.DeviceIdType.MESH
F32 = jnp.float32
BF16 = jnp.bfloat16


def dot(a, b):
    return lax.dot_general(a, b, (((1,), (0,)), ((), ())), preferred_element_type=F32)


def dot_t(a, b):
    return lax.dot_general(a, b, (((1,), (1,)), ((), ())), preferred_element_type=F32)


def lane_sums(x):
    s = jnp.sum(x, axis=0, keepdims=True)
    return functools.reduce(jnp.add, [s[:, i : i + 128] for i in range(0, s.shape[1], 128)])


def block_sizes(rows, order):
    wide = min(order // 2, 512)
    return wide, 2 if rows % 256 == 0 and wide % (2 * rows) == 0 else 1


def kernel(
    n, nf, weight, data, *refs,
):
    models, image, coef, refs = refs[:ITERS], refs[ITERS], refs[ITERS + 1], refs[ITERS + 2 :]
    (
        full, va, vd, va_turned, vd_turned, d_raw, work, early, norms,
        stats, slots, sums, fslots, spot, seats,
        load_sem, ssem, rsem, sum_sem, cast_s, cast_r,
    ) = refs
    m_raw = models[0]
    rows, order = data.shape[2], data.shape[3]
    m = n // 2
    me = lax.axis_index("row")
    mf = lax.axis_index("freq")
    z, c = lax.div(me, 2), lax.rem(me, 2)
    sibling = z * 2 + (1 - c)
    wide, parts = block_sizes(rows, order)
    half = rows // parts
    count = order // wide
    overlap = rows % 128 == 0
    unit = 2 * half if overlap else min(order, 256)
    shadow = overlap and m >= 4
    edge = (z == 0) | (z == m - 1)
    voters = range(2, n - 2) if shadow else range(n)
    votes = (me >= voters[0]) & (me <= voters[-1])

    def at_row(r):
        return {"row": r}

    def wrap(x, size):
        return jnp.where(x >= size, x - size, x)

    def block(i):
        return pl.ds(pl.multiple_of(i * wide, wide), wide)

    def piece(zb, cc, h, p):
        start = pl.multiple_of(((zb * parts + h) * 2 + cc) * half, half)
        return full.at[p, pl.ds(start, half), :]

    def band_columns(u):
        if parts == 1:
            return [pl.ds(pl.multiple_of(u * unit, unit), unit)]
        base = lax.div(u, 2) * 2 * rows + lax.rem(u, 2) * half
        return [pl.ds(pl.multiple_of(base + cc * rows, half), half) for cc in range(2)]

    def regroup(x):
        if parts == 1:
            return x
        group = 2 * rows
        return jnp.concatenate(
            [
                x[:, g + k * half : g + (k + 1) * half]
                for g in range(0, x.shape[1], group)
                for k in (0, 2, 1, 3)
            ],
            axis=1,
        )

    loads = []
    for h in range(parts):
        for p in range(2):
            loads.append(
                pltpu.make_async_copy(
                    data.at[0, p, pl.ds(h * half, half), :],
                    piece(z, c, h, p), load_sem.at[h * 2 + p],
                )
            )
    for p in range(2):
        loads.append(
            pltpu.make_async_copy(
                data.at[0, p], vd.at[pl.ds(p * rows, rows), :], load_sem.at[2 * parts + p]
            )
        )
    for copy in loads:
        copy.start()

    barrier = pltpu.get_barrier_semaphore()

    @pl.loop(1, n)
    def _(k):
        pl.semaphore_signal(
            barrier, inc=1, device_id=at_row(wrap(me + k, n)), device_id_type=MESH
        )

    @pl.loop(1, nf)
    def _(k):
        pl.semaphore_signal(
            barrier, inc=1, device_id={"freq": wrap(mf + k, nf)}, device_id_type=MESH
        )

    stats[...] = jnp.zeros_like(stats)
    for copy in loads[: 2 * parts]:
        copy.wait()
    pl.semaphore_wait(barrier, n - 1 + nf - 1)

    def row_stat(j, seat):
        return pltpu.make_async_remote_copy(
            src_ref=stats.at[0], dst_ref=slots.at[seat], send_sem=sum_sem.at[0],
            recv_sem=sum_sem.at[1], device_id=at_row(j), device_id_type=MESH,
        )

    def freq_stat(j, seat):
        return pltpu.make_async_remote_copy(
            src_ref=sums, dst_ref=fslots.at[seat], send_sem=sum_sem.at[2],
            recv_sem=sum_sem.at[3], device_id={"freq": j}, device_id_type=MESH,
        )

    def bulk(ref, send_sem, recv_sem):
        return pltpu.make_async_remote_copy(
            src_ref=ref, dst_ref=ref, send_sem=send_sem, recv_sem=recv_sem,
            device_id=at_row(sibling), device_id_type=MESH,
        )

    def rows_bulk():
        return bulk(slots.at[pl.ds(0, n - 1)], sum_sem.at[0], sum_sem.at[1])

    def freqs_bulk():
        return bulk(fslots.at[pl.ds(0, nf - 1)], sum_sem.at[2], sum_sem.at[3])

    def start_sum():
        slots[me] = stats[0]

        @pl.loop(1, n)
        def _(i):
            row_stat(wrap(me + i, n), me).start()

    def finish_sum():
        rows_bulk().wait_recv()
        total = jnp.sum(slots[...], axis=0)
        sums[...] = total
        fslots[mf] = total

        @pl.loop(1, nf)
        def _(i):
            freq_stat(wrap(mf + i, nf), mf).start()

        freqs_bulk().wait_recv()
        return jnp.sum(jnp.sum(fslots[...], axis=0), axis=1, keepdims=True)[0:1]

    def drain_sum():
        rows_bulk().wait_send()
        freqs_bulk().wait_send()

    def cast(k, j, g):
        return pltpu.make_async_remote_copy(
            src_ref=spot.at[k], dst_ref=seats.at[k, me * nf + mf],
            send_sem=cast_s.at[k], recv_sem=cast_r.at[k],
            device_id={"row": j, "freq": g}, device_id_type=MESH,
        )

    def cast_bulk(k, number):
        return bulk(seats.at[k, pl.ds(0, number)], cast_s.at[k], cast_r.at[k])

    def others(body):
        @pl.loop(0, n)
        def _(i):
            j = wrap(me + i, n)
            for e in range(nf):
                if e:
                    body(j, wrap(mf + e, nf))
                else:
                    pl.when(i > 0)(lambda: body(j, mf))

    def start_cast(k):
        values = jnp.sum(stats[k + 1], axis=1, keepdims=True)
        lane = lax.broadcasted_iota(jnp.int32, (1, 128), 1)
        spot[k] = jnp.where(lane < 64, values[0:1], values[1:2])
        seats[k, me * nf + mf] = spot[k]
        others(lambda j, g: cast(k, j, g).start())

    def finish_cast(k, members):
        number = len(members) * nf
        if number == n * nf:
            cast_bulk(k, number - 1).wait_recv()
        else:
            pl.when(votes)(lambda: cast_bulk(k, number - 1).wait_recv())
            pl.when(jnp.logical_not(votes))(lambda: cast_bulk(k, number).wait_recv())

        held = seats[k, members[0] * nf : (members[-1] + 1) * nf]
        total = jnp.sum(held, axis=0)
        return total[:, 0:1], total[:, 64:65]

    def drain_cast(k):
        cast_bulk(k, n * nf - 1).wait_send()

    def block_copy(lane, zb, cc, h, p, target):
        return pltpu.make_async_remote_copy(
            src_ref=piece(zb, cc, h, p), dst_ref=piece(zb, cc, h, p),
            send_sem=ssem.at[lane], recv_sem=rsem.at[zb * 2 + cc, h, p],
            device_id=at_row(target), device_id_type=MESH,
        )

    above_me, below_me = wrap(me + 2, n), wrap(me + n - 2, n)

    def spread(zb, h, p, up, down):
        if up:
            @pl.when(z + 1 < m)
            def _():
                block_copy(0, zb, c, h, p, above_me).start()

        if down:
            @pl.when(z > 0)
            def _():
                block_copy(1, zb, c, h, p, below_me).start()

        block_copy(2, zb, c, h, p, sibling).start()

    def settle():
        def sent(lane, blocks):
            bulk(full.at[0, pl.ds(0, 2 * rows * blocks), :], ssem.at[lane], ssem.at[lane]).wait_send()

        for k in range(m):
            @pl.when(z == k)
            def _():
                if k < m - 1:
                    sent(0, k + 1)
                if k > 0:
                    sent(1, m - k)

        sent(2, m)

    def await_piece(zb, cc, h, p):
        block_copy(0, zb, cc, h, p, sibling).wait_recv()

    for p in range(2):
        spread(z, 0, p, True, True)
    for copy in loads[2 * parts :]:
        copy.wait()

    def keep_data(columns, x):
        vd[:, columns] = x
        vd_turned[:rows, columns] = x[rows:]
        vd_turned[rows:, columns] = -x[:rows]

    def keep_model(columns, x):
        va[:, columns] = x
        va_turned[:rows, columns] = -x[rows:]
        va_turned[rows:, columns] = x[:rows]

    @pl.loop(0, count)
    def _(i):
        x = vd[:, block(i)]
        vd_turned[:rows, block(i)] = x[rows:]
        vd_turned[rows:, block(i)] = -x[:rows]
        x = x.astype(F32)
        stats[0, 0:1, :] += lane_sums(x * x)

    start_sum()
    for h in range(1, parts):
        for p in range(2):
            spread(z, h, p, True, True)

    @pl.loop(0, count)
    def _(i):
        work[:, block(i)] = jnp.zeros((2 * rows, wide), F32)

    beta = jnp.sqrt(finish_sum())

    def forward_fit(low, columns):
        return dot(va[:, low], full[0, low, columns]) + dot(va_turned[:, low], full[1, low, columns])

    def adjoint_fit(band):
        return dot_t(vd[...], full[0, band, :]) + dot_t(vd_turned[...], full[1, band, :])

    def gather_columns(ref, slices):
        return jnp.concatenate([ref[:, s] for s in slices], axis=1)

    def begin(u):
        band = pl.ds(pl.multiple_of(u * unit, unit), unit)
        early[...] = dot_t(vd[...], full[0, band, :])

    def process(u, leave, split=False):
        band = pl.ds(pl.multiple_of(u * unit, unit), unit)
        slices = band_columns(u)
        fit = early[...] + dot_t(vd_turned[...], full[1, band, :]) if split else adjoint_fit(band)
        raw = (gather_columns(vd, slices).astype(F32) - weight * fit) / beta
        width = raw.shape[1] // len(slices)
        for k, columns in enumerate(slices):
            m_raw[:, columns] = raw[:, k * width : (k + 1) * width]
        stats[1, 0:1, :] += lane_sums(raw * raw)
        keep_model(band, raw.astype(BF16))

        def visit(i):
            leave(i, work[:, block(i)] + forward_fit(band, block(i)))

        if split:
            for i in range(count):
                visit(i)
        else:
            pl.loop(0, count)(visit)

    def keep_work(i, value):
        work[:, block(i)] = value

    def update_data(it, alpha, beta, i, fit):
        columns = block(i)
        old = vd[:, columns].astype(F32) if it == 0 else d_raw[:, columns]
        new = (models[it][:, columns] - weight * fit) * (1.0 / alpha) - (alpha / beta) * old
        d_raw[:, columns] = new
        keep_data(columns, new.astype(BF16))
        stats[2 * it + 2, 0:1, :] += lane_sums(new * new)

    @pl.loop(0, m - 1 if shadow else m)
    def _(s):
        for h in range(parts):
            @pl.when(s > 0)
            def _():
                for p in range(2):
                    @pl.when(z - s >= 0)
                    def _():
                        await_piece(z - s, c, h, p)
                        spread(z - s, h, p, True, False)

                    @pl.when(z + s < m)
                    def _():
                        await_piece(z + s, c, h, p)
                        spread(z + s, h, p, False, True)

            @pl.loop(0, 2)
            def _(up):
                zb = z - s + 2 * s * up

                @pl.when((zb >= 0) & (zb < m) & ((s > 0) | (up == 0)))
                def _():
                    for p in range(2):
                        await_piece(zb, 1 - c, h, p)
                    if overlap:
                        process(zb * parts + h, keep_work)

    if not overlap:
        @pl.loop(0, order // unit)
        def _(u):
            process(u, keep_work)

    def first_alpha():
        alpha = jnp.sqrt(finish_cast(0, voters)[0])
        norms[0:1, :] = jnp.broadcast_to(alpha, (1, 128))
        return alpha

    def update_all():
        alpha = first_alpha()

        @pl.loop(0, count)
        def _(i):
            update_data(0, alpha, beta, i, work[:, block(i)])

    if shadow:
        @pl.when(jnp.logical_not(edge))
        def _():
            @pl.when((z == 1) | (z == m - 2))
            def _():
                home = jnp.where(z == 1, 0, m - 1)
                if parts == 1:
                    mine = [(home * 2 + c) * rows]
                    high = rows
                else:
                    mine = [(home * parts + c) * unit]
                    high = unit
                mine = [pl.ds(pl.multiple_of(x, high), high) for x in mine]
                for low in mine:
                    @pl.loop(0, order // unit)
                    def _(u):
                        band = pl.ds(pl.multiple_of(u * unit, unit), unit)
                        slices = band_columns(u)
                        for p in range(2):
                            fit = dot_t(full[p, low, :], full[0, band, :])
                            other = dot_t(full[1 - p, low, :], full[1, band, :])
                            fit = fit - other if p else fit + other
                            x = jnp.concatenate([full[p, low, s] for s in slices], axis=1)
                            raw = (x.astype(F32) - weight * fit) / beta
                            stats[1, 0:1, :] += lane_sums(raw * raw)

            start_cast(0)
            update_all()

        @pl.when(edge)
        def _():
            zb = m - 1 - z
            for h in range(parts):
                u = zb * parts + h
                for p in range(2):
                    await_piece(zb, c, h, p)
                    block_copy(2, zb, c, h, p, sibling).start()
                    await_piece(zb, 1 - c, h, p)
                    if p == 0 and h == parts - 1:
                        begin(u)
                if h < parts - 1:
                    process(u, keep_work)
                else:
                    alpha = first_alpha()
                    process(u, functools.partial(update_data, 0, alpha, beta), True)
    else:
        start_cast(0)
        update_all()

    alpha = norms[0:1, 0:1]
    phi_bar, rho_bar = beta, alpha
    direction, answer = [1.0 / alpha], []
    everyone = range(n)
    lead = count - 1
    for it in range(ITERS):
        last = it == ITERS - 1
        ka, kb = 2 * it, 2 * it + 1
        model_ref = models[it]
        low = pl.ds(0, order)

        if it > 0:
            @pl.loop(0, lead)
            def _(i):
                work[:, block(i)] = forward_fit(low, block(i))

            alpha = jnp.sqrt(finish_cast(ka, everyone)[0])
            for i in range(lead, count):
                fit = forward_fit(low, block(i))
                for j in range(i * lead // count if i < count - 1 else 0, lead):
                    update_data(it, alpha, beta, j, work[:, block(j)])
                update_data(it, alpha, beta, i, fit)
            rotate(alpha)
        start_cast(kb)

        def adjoint_image(i):
            return d_raw[:, block(i)] - weight * regroup(adjoint_fit(block(i)))

        if last:
            @pl.loop(0, count)
            def _(i):
                new = adjoint_image(i)
                image[:, block(i)] = new
                stats[kb + 2, 0:1, :] += lane_sums(new * new)
                stats[kb + 2, 1:2, :] += lane_sums(new * model_ref[:, block(i)])

            start_cast(kb + 1)
        else:
            @pl.loop(0, lead)
            def _(i):
                image[:, block(i)] = adjoint_image(i)

        data_sq = finish_cast(kb, everyone)[0]
        beta = jnp.sqrt(data_sq)
        inv_beta, shift = 1.0 / beta, beta / alpha

        if not last:
            def update_model(i, value):
                new = value * inv_beta - shift * model_ref[:, block(i)]
                models[it + 1][:, block(i)] = new
                keep_model(block(i), regroup(new.astype(BF16)))
                stats[kb + 2, 0:1, :] += lane_sums(new * new)

            value = adjoint_image(lead)
            for j in range(lead):
                update_model(j, image[:, block(j)])
            update_model(lead, value)
            start_cast(kb + 1)

        rho = jnp.sqrt(rho_bar * rho_bar + beta * beta)
        cosine, sine = rho_bar / rho, beta / rho
        step = cosine * phi_bar / rho
        phi_bar = sine * phi_bar
        answer = [x + step * w for x, w in zip(answer + [0.0], direction)]

        def rotate(alpha, sine=sine, cosine=cosine, rho=rho):
            nonlocal rho_bar, direction
            rho_bar = -cosine * alpha
            turn = sine * alpha / rho
            direction = [-turn * w for w in direction] + [1.0 / alpha]

    @pl.loop(0, count)
    def _(i):
        basis = [model[:, block(i)] for model in models]
        models[0][:, block(i)] = sum(w * x for w, x in zip(answer, basis))
        models[1][:, block(i)] = sum(w * x for w, x in zip(direction, basis))
        image[:, block(i)] = inv_beta * image[:, block(i)] - shift * basis[-1]

    drain_sum()
    pl.when(votes)(lambda: drain_cast(0))
    for k in range(1, 2 * ITERS):
        drain_cast(k)

    settle()

    image_sq, cross = finish_cast(2 * ITERS, everyone)
    new_alpha = jnp.sqrt(image_sq / data_sq - 2.0 * cross / alpha + data_sq)
    coef[0:1, :] = jnp.broadcast_to(-sine * new_alpha / rho, (1, 128))
    coef[1:2, :] = jnp.broadcast_to(1.0 / new_alpha, (1, 128))
    drain_cast(2 * ITERS)


def combine(coef, ready, turned, fresh, answer, direction, staged, sem):
    rows, order = answer.shape[2], answer.shape[3]
    high = min(rows, 64)
    per = rows // high

    def leave(o, p, i):
        source, out = ((ready, answer), (staged, direction))[o]
        return pltpu.make_async_copy(
            source.at[pl.ds(p * rows + i * high, high), :],
            out.at[0, p, pl.ds(i * high, high), :],
            sem.at[o, p, i],
        )

    tiles = [(p, i) for p in range(2) for i in range(per)]
    for p, i in tiles:
        leave(0, p, i).start()
    old, new = coef[0:1, 0:1], coef[1:2, 0:1]
    for p, i in tiles:
        band = pl.ds(p * rows + i * high, high)
        staged[band, :] = old * turned[band, :] + new * fresh[band, :]
        leave(1, p, i).start()
    for p, i in tiles:
        for o in range(2):
            leave(o, p, i).wait()


def on_device(n, nf, data):
    rows, order = data.shape[2], data.shape[3]
    weight = 1.0 / (3.0 * (2.0 * order) ** 0.5)
    wide, parts = block_sizes(rows, order)
    unit = 2 * rows // parts if rows % 128 == 0 else min(order, 256)
    field = pltpu.VMEM((2 * rows, order), F32)
    rounded = pltpu.VMEM((2 * rows, order), BF16)
    tile = pltpu.VMEM((8, 128), F32)
    casts = 1 + 2 * ITERS
    dma = pltpu.SemaphoreType.DMA
    vmem = pl.BlockSpec(memory_space=pltpu.VMEM)
    anywhere = pl.BlockSpec(memory_space=pl.ANY)
    *basis, coef = pl.pallas_call(
        functools.partial(kernel, n, nf, weight),
        out_shape=(field,) * (ITERS + 1) + (tile,),
        in_specs=[anywhere],
        out_specs=(vmem,) * (ITERS + 2),
        scratch_shapes=[
            pltpu.VMEM((2, order, order), BF16),
            rounded, rounded, rounded, rounded, field, field,
            pltpu.VMEM((2 * rows, unit), F32), tile,
            pltpu.VMEM((casts + 1, 8, 128), F32),
            pltpu.VMEM((n, 8, 128), F32), tile, pltpu.VMEM((nf, 8, 128), F32),
            pltpu.VMEM((casts, 1, 128), F32), pltpu.VMEM((casts, n * nf, 1, 128), F32),
            dma((2 * parts + 2,)), dma((3,)), dma((n, parts, 2)),
            dma((4,)), dma((casts,)), dma((casts,)),
        ],
        compiler_params=pltpu.CompilerParams(
            collective_id=0, has_side_effects=True, vmem_limit_bytes=46 * 2**20
        ),
    )(data)
    out = jax.ShapeDtypeStruct(data.shape, F32)
    high = min(rows, 64)
    return pl.pallas_call(
        combine,
        out_shape=(out, out),
        in_specs=[vmem] * (ITERS + 2),
        out_specs=(anywhere, anywhere),
        scratch_shapes=[pltpu.VMEM((2 * rows, order), F32), dma((2, 2, rows // high))],
        compiler_params=pltpu.CompilerParams(vmem_limit_bytes=24 * 2**20),
    )(coef, *basis)


def solution(mesh):
    spec = P("freq", None, "row", None)
    return jax.shard_map(
        functools.partial(on_device, mesh.shape["row"], mesh.shape["freq"]),
        mesh=mesh,
        in_specs=(spec,),
        out_specs=(spec, spec),
        check_vma=False,
    )
```

time: 197 us -> 191 us (0.970)
  Pallas kernels: 196 us -> 190 us
    pallas_call x1, Pallas kernels: 193 us -> 186 us  [on_device(): pl.pallas_call(functools.partial(kernel, n, nf, weight), out_shape=(field...]
where the time goes in v3:
time: 191 us
  Pallas kernels  190 us (99%)
    pallas_call x1, Pallas kernels, on_device(): pl.pallas_call(functools.partial(kernel, n, nf, weight), out_shape=(field...  186 us

profile of v3, /device:TPU:0, one launch (start us, length us, event | category | flops | bytes accessed | tf_op | source)
XLA Modules:
  0.0 190.6 jit_solution(3030952733028647209)
XLA Ops:
  0.6 186.4 %shard_map.30 = (f32[512,2048]{1,0:T(8,128)S(1)}, f32[512,2048]{1,0:T(8,128)S(1)}, f32[512,2048]{1,0:T(8,128)S(1)}, f32[8,128]{1,0:T(8,128)S(1)}) custom-call(bf16[1,2,256,2048]{3,2,1,0:T(8,128)(2,1)} %data.1), custom_call_target="tpu_custom_call" | custom-call | tf_op jit(solution)/shard_map/pallas_call | solution.py:559
  187.0 3.4 %shard_map.31 = (f32[1,2,256,2048]{3,2,1,0:T(8,128)}, f32[1,2,256,2048]{3,2,1,0:T(8,128)}) custom-call(f32[8,128]{1,0:T(8,128)S(1)} %get-tuple-element.6.coef, f32[512,2048]{1,0:T(8,128)S(1)} %get-tuple-element.7.ready, f32[512,2048]{1,0:T(8,128)S(1)} %get-tuple-element.8.turned, f32[512,2048]{1,0:T(8,128)S(1)} %get-tuple-element.9.fresh), custom_call_target="tpu_custom_call" | custom-call | tf_op jit(solution)/shard_map/pallas_call | solution.py:580

commit v4 on v3

--- a/solution.py
+++ b/solution.py
@@ -21,9 +21,15 @@
     return lax.dot_general(a, b, (((1,), (1,)), ((), ())), preferred_element_type=F32)
 
 
-def lane_sums(x):
-    s = jnp.sum(x, axis=0, keepdims=True)
-    return functools.reduce(jnp.add, [s[:, i : i + 128] for i in range(0, s.shape[1], 128)])
+def fold(x):
+    tiles = [
+        x[r : r + 8, i : i + 128]
+        for r in range(0, x.shape[0], 8)
+        for i in range(0, x.shape[1], 128)
+    ]
+    while len(tiles) > 1:
+        tiles = [sum(tiles[k : k + 2][1:], tiles[k]) for k in range(0, len(tiles), 2)]
+    return tiles[0]
 
 
 def block_sizes(rows, order):
@@ -36,7 +42,7 @@
 ):
     models, image, coef, refs = refs[:ITERS], refs[ITERS], refs[ITERS + 1], refs[ITERS + 2 :]
     (
-        full, va, vd, va_turned, vd_turned, d_raw, work, early, norms,
+        full, va, vd, va_turned, vd_turned, d_raw, work, early,
         stats, slots, sums, fslots, spot, seats,
         load_sem, ssem, rsem, sum_sem, cast_s, cast_r,
     ) = refs
@@ -128,7 +134,7 @@
 
     def row_stat(j, seat):
         return pltpu.make_async_remote_copy(
-            src_ref=stats.at[0], dst_ref=slots.at[seat], send_sem=sum_sem.at[0],
+            src_ref=stats.at[0, 0], dst_ref=slots.at[seat], send_sem=sum_sem.at[0],
             recv_sem=sum_sem.at[1], device_id=at_row(j), device_id_type=MESH,
         )
 
@@ -151,7 +157,7 @@
         return bulk(fslots.at[pl.ds(0, nf - 1)], sum_sem.at[2], sum_sem.at[3])
 
     def start_sum():
-        slots[me] = stats[0]
+        slots[me] = stats[0, 0]
 
         @pl.loop(1, n)
         def _(i):
@@ -168,7 +174,8 @@
             freq_stat(wrap(mf + i, nf), mf).start()
 
         freqs_bulk().wait_recv()
-        return jnp.sum(jnp.sum(fslots[...], axis=0), axis=1, keepdims=True)[0:1]
+        total = jnp.sum(jnp.sum(fslots[...], axis=0), axis=0, keepdims=True)
+        return jnp.sum(total, axis=1, keepdims=True)
 
     def drain_sum():
         rows_bulk().wait_send()
@@ -185,19 +192,27 @@
         return bulk(seats.at[k, pl.ds(0, number)], cast_s.at[k], cast_r.at[k])
 
     def others(body):
+        if n * nf <= 64:
+            for i in range(n):
+                for e in range(nf):
+                    if i or e:
+                        body(wrap(me + i, n), wrap(mf + e, nf))
+            return
+
         @pl.loop(0, n)
         def _(i):
             j = wrap(me + i, n)
-            for e in range(nf):
-                if e:
-                    body(j, wrap(mf + e, nf))
-                else:
-                    pl.when(i > 0)(lambda: body(j, mf))
+            pl.when(i > 0)(lambda: body(j, mf))
+            for e in range(1, nf):
+                body(j, wrap(mf + e, nf))
 
     def start_cast(k):
-        values = jnp.sum(stats[k + 1], axis=1, keepdims=True)
+        first, second = [
+            jnp.sum(jnp.sum(stats[k + 1, q], axis=0, keepdims=True), axis=1, keepdims=True)
+            for q in range(2)
+        ]
         lane = lax.broadcasted_iota(jnp.int32, (1, 128), 1)
-        spot[k] = jnp.where(lane < 64, values[0:1], values[1:2])
+        spot[k] = jnp.where(lane < 64, first, second)
         seats[k, me * nf + mf] = spot[k]
         others(lambda j, g: cast(k, j, g).start())
 
@@ -260,24 +275,38 @@
     for copy in loads[2 * parts :]:
         copy.wait()
 
-    def keep_data(columns, x):
-        vd[:, columns] = x
-        vd_turned[:rows, columns] = x[rows:]
-        vd_turned[rows:, columns] = -x[:rows]
-
-    def keep_model(columns, x):
-        va[:, columns] = x
-        va_turned[:rows, columns] = -x[rows:]
-        va_turned[rows:, columns] = x[:rows]
-
-    @pl.loop(0, count)
-    def _(i):
-        x = vd[:, block(i)]
-        vd_turned[:rows, block(i)] = x[rows:]
-        vd_turned[rows:, block(i)] = -x[:rows]
-        x = x.astype(F32)
-        stats[0, 0:1, :] += lane_sums(x * x)
-
+    high = 64 if rows % 64 == 0 else 16
+
+    def sweep(body, stat):
+        @pl.loop(0, rows // high)
+        def _(t):
+            for r in range(0, high, 16):
+                low = pl.multiple_of(t * high + r, 16)
+                for i in range(0, order, wide):
+                    total = body(pl.ds(low, 16), pl.ds(rows + low, 16), pl.ds(i, wide))
+                    if stat is not None:
+                        stats[stat, 0] += total
+
+    def keep_data(real, imag, columns, xr, xi):
+        vd[real, columns] = xr
+        vd[imag, columns] = xi
+        vd_turned[real, columns] = xi
+        vd_turned[imag, columns] = -xr
+
+    def keep_model(real, imag, columns, xr, xi):
+        va[real, columns] = xr
+        va[imag, columns] = xi
+        va_turned[real, columns] = -xi
+        va_turned[imag, columns] = xr
+
+    def first_pass(real, imag, columns):
+        xr, xi = vd[real, columns], vd[imag, columns]
+        vd_turned[real, columns] = xi
+        vd_turned[imag, columns] = -xr
+        xr, xi = xr.astype(F32), xi.astype(F32)
+        return fold(xr * xr + xi * xi)
+
+    sweep(first_pass, 0)
     start_sum()
     for h in range(1, parts):
         for p in range(2):
@@ -288,6 +317,7 @@
         work[:, block(i)] = jnp.zeros((2 * rows, wide), F32)
 
     beta = jnp.sqrt(finish_sum())
+    inv_first = 1.0 / beta
 
     def forward_fit(low, columns):
         return dot(va[:, low], full[0, low, columns]) + dot(va_turned[:, low], full[1, low, columns])
@@ -295,26 +325,40 @@
     def adjoint_fit(band):
         return dot_t(vd[...], full[0, band, :]) + dot_t(vd_turned[...], full[1, band, :])
 
-    def gather_columns(ref, slices):
-        return jnp.concatenate([ref[:, s] for s in slices], axis=1)
+    def band_fit(v, p, band):
+        return jnp.concatenate(
+            [dot_t(v[r : r + rows], full[p, band, :]) for r in (0, rows)], axis=0
+        )
 
     def begin(u):
         band = pl.ds(pl.multiple_of(u * unit, unit), unit)
-        early[...] = dot_t(vd[...], full[0, band, :])
-
-    def process(u, leave, split=False):
+        early[...] = band_fit(vd, 0, band)
+
+    def process(u, split=False):
         band = pl.ds(pl.multiple_of(u * unit, unit), unit)
         slices = band_columns(u)
-        fit = early[...] + dot_t(vd_turned[...], full[1, band, :]) if split else adjoint_fit(band)
-        raw = (gather_columns(vd, slices).astype(F32) - weight * fit) / beta
-        width = raw.shape[1] // len(slices)
-        for k, columns in enumerate(slices):
-            m_raw[:, columns] = raw[:, k * width : (k + 1) * width]
-        stats[1, 0:1, :] += lane_sums(raw * raw)
-        keep_model(band, raw.astype(BF16))
+        fit = early[...] if split else band_fit(vd, 0, band)
+        fit += band_fit(vd_turned, 1, band)
+        width = unit // len(slices)
+        total = jnp.zeros((8, 128), F32)
+        for r in range(0, rows, 16):
+            pair = pl.ds(r, 16), pl.ds(rows + r, 16)
+            rounded = []
+            for side in pair:
+                pieces = []
+                for k, columns in enumerate(slices):
+                    x = fit[side.start : side.start + 16, k * width : (k + 1) * width]
+                    x = (vd[side, columns].astype(F32) - weight * x) * inv_first
+                    m_raw[side, columns] = x
+                    work[side, columns] += x
+                    total += fold(x * x)
+                    pieces.append(x.astype(BF16))
+                rounded.append(jnp.concatenate(pieces, axis=1))
+            keep_model(*pair, band, *rounded)
+        stats[1, 0] += total
 
         def visit(i):
-            leave(i, work[:, block(i)] + forward_fit(band, block(i)))
+            work[:, block(i)] -= weight * forward_fit(band, block(i))
 
         if split:
             for i in range(count):
@@ -322,16 +366,19 @@
         else:
             pl.loop(0, count)(visit)
 
-    def keep_work(i, value):
-        work[:, block(i)] = value
-
-    def update_data(it, alpha, beta, i, fit):
-        columns = block(i)
-        old = vd[:, columns].astype(F32) if it == 0 else d_raw[:, columns]
-        new = (models[it][:, columns] - weight * fit) * (1.0 / alpha) - (alpha / beta) * old
-        d_raw[:, columns] = new
-        keep_data(columns, new.astype(BF16))
-        stats[2 * it + 2, 0:1, :] += lane_sums(new * new)
+    def update_data(it, alpha, beta):
+        inv_alpha, keep = 1.0 / alpha, alpha / beta
+
+        def body(real, imag, columns):
+            new = []
+            for side in (real, imag):
+                old = vd[side, columns].astype(F32) if it == 0 else d_raw[side, columns]
+                new.append(work[side, columns] * inv_alpha - keep * old)
+                d_raw[side, columns] = new[-1]
+            keep_data(real, imag, columns, *[x.astype(BF16) for x in new])
+            return fold(new[0] * new[0] + new[1] * new[1])
+
+        sweep(body, 2 * it + 2)
 
     @pl.loop(0, m - 1 if shadow else m)
     def _(s):
@@ -358,24 +405,12 @@
                     for p in range(2):
                         await_piece(zb, 1 - c, h, p)
                     if overlap:
-                        process(zb * parts + h, keep_work)
+                        process(zb * parts + h)
 
     if not overlap:
         @pl.loop(0, order // unit)
         def _(u):
-            process(u, keep_work)
-
-    def first_alpha():
-        alpha = jnp.sqrt(finish_cast(0, voters)[0])
-        norms[0:1, :] = jnp.broadcast_to(alpha, (1, 128))
-        return alpha
-
-    def update_all():
-        alpha = first_alpha()
-
-        @pl.loop(0, count)
-        def _(i):
-            update_data(0, alpha, beta, i, work[:, block(i)])
+            process(u)
 
     if shadow:
         @pl.when(jnp.logical_not(edge))
@@ -400,11 +435,10 @@
                             other = dot_t(full[1 - p, low, :], full[1, band, :])
                             fit = fit - other if p else fit + other
                             x = jnp.concatenate([full[p, low, s] for s in slices], axis=1)
-                            raw = (x.astype(F32) - weight * fit) / beta
-                            stats[1, 0:1, :] += lane_sums(raw * raw)
+                            raw = (x.astype(F32) - weight * fit) * inv_first
+                            stats[1, 0] += fold(raw * raw)
 
             start_cast(0)
-            update_all()
 
         @pl.when(edge)
         def _():
@@ -417,72 +451,63 @@
                     await_piece(zb, 1 - c, h, p)
                     if p == 0 and h == parts - 1:
                         begin(u)
-                if h < parts - 1:
-                    process(u, keep_work)
-                else:
-                    alpha = first_alpha()
-                    process(u, functools.partial(update_data, 0, alpha, beta), True)
+                process(u, h == parts - 1)
     else:
         start_cast(0)
-        update_all()
-
-    alpha = norms[0:1, 0:1]
+
+    alpha = jnp.sqrt(finish_cast(0, voters)[0])
     phi_bar, rho_bar = beta, alpha
     direction, answer = [1.0 / alpha], []
     everyone = range(n)
-    lead = count - 1
     for it in range(ITERS):
         last = it == ITERS - 1
         ka, kb = 2 * it, 2 * it + 1
         model_ref = models[it]
-        low = pl.ds(0, order)
 
         if it > 0:
-            @pl.loop(0, lead)
-            def _(i):
-                work[:, block(i)] = forward_fit(low, block(i))
-
-            alpha = jnp.sqrt(finish_cast(ka, everyone)[0])
-            for i in range(lead, count):
-                fit = forward_fit(low, block(i))
-                for j in range(i * lead // count if i < count - 1 else 0, lead):
-                    update_data(it, alpha, beta, j, work[:, block(j)])
-                update_data(it, alpha, beta, i, fit)
-            rotate(alpha)
-        start_cast(kb)
-
-        def adjoint_image(i):
-            return d_raw[:, block(i)] - weight * regroup(adjoint_fit(block(i)))
-
-        if last:
             @pl.loop(0, count)
             def _(i):
-                new = adjoint_image(i)
-                image[:, block(i)] = new
-                stats[kb + 2, 0:1, :] += lane_sums(new * new)
-                stats[kb + 2, 1:2, :] += lane_sums(new * model_ref[:, block(i)])
-
+                fit = forward_fit(pl.ds(0, order), block(i))
+                work[:, block(i)] = model_ref[:, block(i)] - weight * fit
+
+            alpha = jnp.sqrt(finish_cast(ka, everyone)[0])
+            rotate(alpha)
+        update_data(it, alpha, beta)
+        start_cast(kb)
+
+        @pl.loop(0, count)
+        def _(i):
+            image[:, block(i)] = d_raw[:, block(i)] - weight * regroup(adjoint_fit(block(i)))
+
+        if last:
+            def squares(real, imag, columns):
+                xr, xi = image[real, columns], image[imag, columns]
+                return fold(xr * xr + xi * xi)
+
+            def products(real, imag, columns):
+                stats[kb + 2, 1] += fold(
+                    image[real, columns] * model_ref[real, columns]
+                    + image[imag, columns] * model_ref[imag, columns]
+                )
+                return squares(real, imag, columns)
+
+            sweep(products, kb + 2)
             start_cast(kb + 1)
-        else:
-            @pl.loop(0, lead)
-            def _(i):
-                image[:, block(i)] = adjoint_image(i)
 
         data_sq = finish_cast(kb, everyone)[0]
         beta = jnp.sqrt(data_sq)
         inv_beta, shift = 1.0 / beta, beta / alpha
 
         if not last:
-            def update_model(i, value):
-                new = value * inv_beta - shift * model_ref[:, block(i)]
-                models[it + 1][:, block(i)] = new
-                keep_model(block(i), regroup(new.astype(BF16)))
-                stats[kb + 2, 0:1, :] += lane_sums(new * new)
-
-            value = adjoint_image(lead)
-            for j in range(lead):
-                update_model(j, image[:, block(j)])
-            update_model(lead, value)
+            def update_model(real, imag, columns):
+                new = []
+                for side in (real, imag):
+                    new.append(image[side, columns] * inv_beta - shift * model_ref[side, columns])
+                    models[it + 1][side, columns] = new[-1]
+                keep_model(real, imag, columns, *[regroup(x.astype(BF16)) for x in new])
+                return fold(new[0] * new[0] + new[1] * new[1])
+
+            sweep(update_model, kb + 2)
             start_cast(kb + 1)
 
         rho = jnp.sqrt(rho_bar * rho_bar + beta * beta)
@@ -497,13 +522,15 @@
             turn = sine * alpha / rho
             direction = [-turn * w for w in direction] + [1.0 / alpha]
 
-    @pl.loop(0, count)
-    def _(i):
-        basis = [model[:, block(i)] for model in models]
-        models[0][:, block(i)] = sum(w * x for w, x in zip(answer, basis))
-        models[1][:, block(i)] = sum(w * x for w, x in zip(direction, basis))
-        image[:, block(i)] = inv_beta * image[:, block(i)] - shift * basis[-1]
-
+    def combine_basis(real, imag, columns):
+        for side in (real, imag):
+            basis = [model[side, columns] for model in models]
+            fresh = image[side, columns]
+            models[0][side, columns] = sum(w * x for w, x in zip(answer[1:], basis[1:])) + answer[0] * basis[0]
+            models[1][side, columns] = sum(w * x for w, x in zip(direction[1:], basis[1:])) + direction[0] * basis[0]
+            image[side, columns] = inv_beta * fresh - shift * basis[-1]
+
+    sweep(combine_basis, None)
     drain_sum()
     pl.when(votes)(lambda: drain_cast(0))
     for k in range(1, 2 * ITERS):
@@ -564,8 +591,8 @@
         scratch_shapes=[
             pltpu.VMEM((2, order, order), BF16),
             rounded, rounded, rounded, rounded, field, field,
-            pltpu.VMEM((2 * rows, unit), F32), tile,
-            pltpu.VMEM((casts + 1, 8, 128), F32),
+            pltpu.VMEM((2 * rows, unit), F32),
+            pltpu.VMEM((casts + 1, 2, 8, 128), F32),
             pltpu.VMEM((n, 8, 128), F32), tile, pltpu.VMEM((nf, 8, 128), F32),
             pltpu.VMEM((casts, 1, 128), F32), pltpu.VMEM((casts, n * nf, 1, 128), F32),
             dma((2 * parts + 2,)), dma((3,)), dma((n, parts, 2)),

time: 191 us -> 189 us (0.990)
  Pallas kernels: 190 us -> 188 us
where the time goes in v4:
time: 189 us
  Pallas kernels  188 us (99%)
    pallas_call x1, Pallas kernels, on_device(): pl.pallas_call(functools.partial(kernel, n, nf, weight), out_shape=(field...  185 us

profile of v4, /device:TPU:0, one launch (start us, length us, event | category | flops | bytes accessed | tf_op | source)
XLA Modules:
  0.0 188.9 jit_solution(11186761390303352938)
XLA Ops:
  0.6 184.7 %shard_map.30 = (f32[512,2048]{1,0:T(8,128)S(1)}, f32[512,2048]{1,0:T(8,128)S(1)}, f32[512,2048]{1,0:T(8,128)S(1)}, f32[8,128]{1,0:T(8,128)S(1)}) custom-call(bf16[1,2,256,2048]{3,2,1,0:T(8,128)(2,1)} %data.1), custom_call_target="tpu_custom_call" | custom-call | tf_op jit(solution)/shard_map/pallas_call | solution.py:586
  185.3 3.4 %shard_map.31 = (f32[1,2,256,2048]{3,2,1,0:T(8,128)}, f32[1,2,256,2048]{3,2,1,0:T(8,128)}) custom-call(f32[8,128]{1,0:T(8,128)S(1)} %get-tuple-element.6.coef, f32[512,2048]{1,0:T(8,128)S(1)} %get-tuple-element.7.ready, f32[512,2048]{1,0:T(8,128)S(1)} %get-tuple-element.8.turned, f32[512,2048]{1,0:T(8,128)S(1)} %get-tuple-element.9.fresh), custom_call_target="tpu_custom_call" | custom-call | tf_op jit(solution)/shard_map/pallas_call | solution.py:607

commit v5 on v4

--- a/solution.py
+++ b/solution.py
@@ -277,6 +277,14 @@
 
     high = 64 if rows % 64 == 0 else 16
 
+    def tiles(body, stat, done):
+        for i in done:
+            total = jnp.zeros((8, 128), F32)
+            for r in range(0, rows, 16):
+                part = body(pl.ds(r, 16), pl.ds(rows + r, 16), pl.ds(i * wide, wide))
+                total += part
+            stats[stat, 0] += total
+
     def sweep(body, stat):
         @pl.loop(0, rows // high)
         def _(t):
@@ -378,7 +386,7 @@
             keep_data(real, imag, columns, *[x.astype(BF16) for x in new])
             return fold(new[0] * new[0] + new[1] * new[1])
 
-        sweep(body, 2 * it + 2)
+        return body
 
     @pl.loop(0, m - 1 if shadow else m)
     def _(s):
@@ -464,35 +472,40 @@
         ka, kb = 2 * it, 2 * it + 1
         model_ref = models[it]
 
+        def forward_block(i):
+            fit = forward_fit(pl.ds(0, order), block(i))
+            work[:, block(i)] = model_ref[:, block(i)] - weight * fit
+
+        def adjoint_block(i):
+            image[:, block(i)] = d_raw[:, block(i)] - weight * regroup(adjoint_fit(block(i)))
+
         if it > 0:
-            @pl.loop(0, count)
-            def _(i):
-                fit = forward_fit(pl.ds(0, order), block(i))
-                work[:, block(i)] = model_ref[:, block(i)] - weight * fit
-
+            for i in range(count - 1):
+                forward_block(i)
             alpha = jnp.sqrt(finish_cast(ka, everyone)[0])
             rotate(alpha)
-        update_data(it, alpha, beta)
+            body = update_data(it, alpha, beta)
+            tiles(body, kb + 1, range(count - 1))
+            forward_block(count - 1)
+            tiles(body, kb + 1, range(count - 1, count))
+        else:
+            sweep(update_data(it, alpha, beta), kb + 1)
         start_cast(kb)
 
-        @pl.loop(0, count)
-        def _(i):
-            image[:, block(i)] = d_raw[:, block(i)] - weight * regroup(adjoint_fit(block(i)))
-
         if last:
-            def squares(real, imag, columns):
+            def products(real, imag, columns):
                 xr, xi = image[real, columns], image[imag, columns]
+                stats[kb + 2, 1] += fold(xr * model_ref[real, columns] + xi * model_ref[imag, columns])
                 return fold(xr * xr + xi * xi)
 
-            def products(real, imag, columns):
-                stats[kb + 2, 1] += fold(
-                    image[real, columns] * model_ref[real, columns]
-                    + image[imag, columns] * model_ref[imag, columns]
-                )
-                return squares(real, imag, columns)
-
-            sweep(products, kb + 2)
+            for i in range(count):
+                adjoint_block(i)
+                tiles(products, kb + 2, range(i - 1, i) if i else ())
+            tiles(products, kb + 2, range(count - 1, count))
             start_cast(kb + 1)
+        else:
+            for i in range(count - 1):
+                adjoint_block(i)
 
         data_sq = finish_cast(kb, everyone)[0]
         beta = jnp.sqrt(data_sq)
@@ -507,7 +520,9 @@
                 keep_model(real, imag, columns, *[regroup(x.astype(BF16)) for x in new])
                 return fold(new[0] * new[0] + new[1] * new[1])
 
-            sweep(update_model, kb + 2)
+            tiles(update_model, kb + 2, range(count - 1))
+            adjoint_block(count - 1)
+            tiles(update_model, kb + 2, range(count - 1, count))
             start_cast(kb + 1)
 
         rho = jnp.sqrt(rho_bar * rho_bar + beta * beta)

time: 189 us -> 187 us (0.989)
  Pallas kernels: 188 us -> 186 us
where the time goes in v5:
time: 187 us
  Pallas kernels  186 us (99%)
    pallas_call x1, Pallas kernels, on_device(): pl.pallas_call(functools.partial(kernel, n, nf, weight), out_shape=(field...  183 us

profile of v5, /device:TPU:0, one launch (start us, length us, event | category | flops | bytes accessed | tf_op | source)
XLA Modules:
  0.0 187.1 jit_solution(8839404580631182508)
XLA Ops:
  0.6 182.9 %shard_map.30 = (f32[512,2048]{1,0:T(8,128)S(1)}, f32[512,2048]{1,0:T(8,128)S(1)}, f32[512,2048]{1,0:T(8,128)S(1)}, f32[8,128]{1,0:T(8,128)S(1)}) custom-call(bf16[1,2,256,2048]{3,2,1,0:T(8,128)(2,1)} %data.1), custom_call_target="tpu_custom_call" | custom-call | tf_op jit(solution)/shard_map/pallas_call | solution.py:601
  183.5 3.4 %shard_map.31 = (f32[1,2,256,2048]{3,2,1,0:T(8,128)}, f32[1,2,256,2048]{3,2,1,0:T(8,128)}) custom-call(f32[8,128]{1,0:T(8,128)S(1)} %get-tuple-element.6.coef, f32[512,2048]{1,0:T(8,128)S(1)} %get-tuple-element.7.ready, f32[512,2048]{1,0:T(8,128)S(1)} %get-tuple-element.8.turned, f32[512,2048]{1,0:T(8,128)S(1)} %get-tuple-element.9.fresh), custom_call_target="tpu_custom_call" | custom-call | tf_op jit(solution)/shard_map/pallas_call | solution.py:622

commit v6 on v5

--- a/solution.py
+++ b/solution.py
@@ -193,8 +193,8 @@
 
     def others(body):
         if n * nf <= 64:
-            for i in range(n):
-                for e in range(nf):
+            for i in sorted(range(n), key=lambda i: -abs(2 * i - n)):
+                for e in reversed(range(nf)):
                     if i or e:
                         body(wrap(me + i, n), wrap(mf + e, nf))
             return
@@ -216,7 +216,7 @@
         seats[k, me * nf + mf] = spot[k]
         others(lambda j, g: cast(k, j, g).start())
 
-    def finish_cast(k, members):
+    def await_cast(k, members):
         number = len(members) * nf
         if number == n * nf:
             cast_bulk(k, number - 1).wait_recv()
@@ -224,9 +224,14 @@
             pl.when(votes)(lambda: cast_bulk(k, number - 1).wait_recv())
             pl.when(jnp.logical_not(votes))(lambda: cast_bulk(k, number).wait_recv())
 
+    def read_cast(k, members):
         held = seats[k, members[0] * nf : (members[-1] + 1) * nf]
         total = jnp.sum(held, axis=0)
         return total[:, 0:1], total[:, 64:65]
+
+    def finish_cast(k, members):
+        await_cast(k, members)
+        return read_cast(k, members)
 
     def drain_cast(k):
         cast_bulk(k, n * nf - 1).wait_send()
@@ -275,7 +280,7 @@
     for copy in loads[2 * parts :]:
         copy.wait()
 
-    high = 64 if rows % 64 == 0 else 16
+    high = 128 if rows % 128 == 0 else 16
 
     def tiles(body, stat, done):
         for i in done:
@@ -342,7 +347,7 @@
         band = pl.ds(pl.multiple_of(u * unit, unit), unit)
         early[...] = band_fit(vd, 0, band)
 
-    def process(u, split=False):
+    def process(u, split=False, after=None):
         band = pl.ds(pl.multiple_of(u * unit, unit), unit)
         slices = band_columns(u)
         fit = early[...] if split else band_fit(vd, 0, band)
@@ -371,6 +376,9 @@
         if split:
             for i in range(count):
                 visit(i)
+                if i:
+                    tiles(after, 2, range(i - 1, i))
+            tiles(after, 2, range(count - 1, count))
         else:
             pl.loop(0, count)(visit)
 
@@ -419,6 +427,9 @@
         @pl.loop(0, order // unit)
         def _(u):
             process(u)
+
+    def first_update():
+        return update_data(0, jnp.sqrt(finish_cast(0, voters)[0]), beta)
 
     if shadow:
         @pl.when(jnp.logical_not(edge))
@@ -447,6 +458,7 @@
                             stats[1, 0] += fold(raw * raw)
 
             start_cast(0)
+            sweep(first_update(), 2)
 
         @pl.when(edge)
         def _():
@@ -459,11 +471,15 @@
                     await_piece(zb, 1 - c, h, p)
                     if p == 0 and h == parts - 1:
                         begin(u)
-                process(u, h == parts - 1)
+                if h < parts - 1:
+                    process(u)
+                else:
+                    process(u, True, first_update())
     else:
         start_cast(0)
-
-    alpha = jnp.sqrt(finish_cast(0, voters)[0])
+        sweep(first_update(), 2)
+
+    alpha = jnp.sqrt(read_cast(0, voters)[0])
     phi_bar, rho_bar = beta, alpha
     direction, answer = [1.0 / alpha], []
     everyone = range(n)
@@ -488,8 +504,6 @@
             tiles(body, kb + 1, range(count - 1))
             forward_block(count - 1)
             tiles(body, kb + 1, range(count - 1, count))
-        else:
-            sweep(update_data(it, alpha, beta), kb + 1)
         start_cast(kb)
 
         if last:

time: 187 us -> 187 us (level)
  no operation moved by 1% of the time
where the time goes in v6:
time: 187 us
  Pallas kernels  186 us (99%)
    pallas_call x1, Pallas kernels, on_device(): pl.pallas_call(functools.partial(kernel, n, nf, weight), out_shape=(field...  182 us

profile of v6, /device:TPU:0, one launch (start us, length us, event | category | flops | bytes accessed | tf_op | source)
XLA Modules:
  0.0 186.7 jit_solution(6711825961202515101)
XLA Ops:
  0.6 182.5 %shard_map.30 = (f32[512,2048]{1,0:T(8,128)S(1)}, f32[512,2048]{1,0:T(8,128)S(1)}, f32[512,2048]{1,0:T(8,128)S(1)}, f32[8,128]{1,0:T(8,128)S(1)}) custom-call(bf16[1,2,256,2048]{3,2,1,0:T(8,128)(2,1)} %data.1), custom_call_target="tpu_custom_call" | custom-call | tf_op jit(solution)/shard_map/pallas_call | solution.py:615
  183.1 3.4 %shard_map.31 = (f32[1,2,256,2048]{3,2,1,0:T(8,128)}, f32[1,2,256,2048]{3,2,1,0:T(8,128)}) custom-call(f32[8,128]{1,0:T(8,128)S(1)} %get-tuple-element.6.coef, f32[512,2048]{1,0:T(8,128)S(1)} %get-tuple-element.7.ready, f32[512,2048]{1,0:T(8,128)S(1)} %get-tuple-element.8.turned, f32[512,2048]{1,0:T(8,128)S(1)} %get-tuple-element.9.fresh), custom_call_target="tpu_custom_call" | custom-call | tf_op jit(solution)/shard_map/pallas_call | solution.py:636
